TPU v7x, 128 devices: a whole 4x4x4 slice. The times are simulated.
128 devices in a mesh: dp: 8 (over y, x_lo), expert: 16 (over x_hi, z, core).
Axes of the slice: x: 4 (x_hi: 2, x_lo: 2; x = x_hi * 2 + x_lo), y: 4, z: 4, core: 2. Of those that a mesh axis runs over, the one named last changes fastest.
Arguments:
- tokens: bfloat16 [40960, 2048], P(('dp', 'expert')), may hold values from -24 to 24
- out_grad: bfloat16 [40960, 2048], P(('dp', 'expert')), may hold values from -24 to 24
- expert_ids: int32 [40960, 2], P(('dp', 'expert')), may hold values from 0 to 15, all different within a row; in each aligned block of 320 rows (0 to 319, 320 to 639, ...) at most 60 rows name the same one
- route_weight: bfloat16 [40960, 2], P(('dp', 'expert')), may hold values from 0.099609375 to 1
- w_gate: bfloat16 [16, 2048, 768], P('expert', 'dp'), may hold values from -0.125 to 0.125
- w_up: bfloat16 [16, 2048, 768], P('expert', 'dp'), may hold values from -0.125 to 0.125
- w_down: bfloat16 [16, 768, 2048], P('expert', None, 'dp'), may hold values from -0.21875 to 0.21875
Outputs:
- token_grad: bfloat16 [40960, 2048], P(('dp', 'expert'))
- route_grad: bfloat16 [40960, 2], P(('dp', 'expert'))
- gate_grad: bfloat16 [16, 2048, 768], P('expert', 'dp')
- up_grad: bfloat16 [16, 2048, 768], P('expert', 'dp')
- down_grad: bfloat16 [16, 768, 2048], P('expert', None, 'dp')
Inputs may be any that keep to these rules, and one draw needn't show every extreme that they name: `expert_ids`: each row names 2 different experts. In the rows of one device no expert is named more than 60 times, a bound that some block reaches in some device.
All inputs are finite; a program needn't handle non-finite values.
Results may differ from a plain program's by a relative error of at most 0.014.
Values may be sent and summed in bfloat16 or wider, within the bound.
A program may use at most 128 MiB of HBM per device.

v0:
```python
import jax
import jax.numpy as jnp
from jax import lax
from jax.sharding import PartitionSpec as P


def side_by_side(arrays, axis, split_dim, concat_dim, along):
    widths = [a.shape[along] for a in arrays]
    both = jnp.concatenate(arrays, axis=along)
    out = lax.all_to_all(both, axis, split_axis=split_dim, concat_axis=concat_dim, tiled=True)
    return tuple(jnp.split(out, [sum(widths[:k]) for k in range(1, len(widths))], axis=along))


def sent_together(arrays, axis, dim, along):
    both = jnp.concatenate(arrays, axis=along)
    out, at, outs = (lax.all_gather(both, axis, axis=dim, tiled=True), 0, [])
    for a in arrays:
        outs.append(lax.slice_in_dim(out, at, at + a.shape[along], axis=along))
        at += a.shape[along]
    return tuple(outs)


def side_by_side_2(arrays, axis, dim, along):
    both = jnp.concatenate(arrays, axis=along)
    out, at, outs = (lax.psum_scatter(both, axis, scatter_dimension=dim, tiled=True), 0, [])
    for a in arrays:
        outs.append(lax.slice_in_dim(out, at, at + a.shape[along], axis=along))
        at += a.shape[along]
    return tuple(outs)


def on_device(tokens, out_grad, expert_ids, route_weight, w_gate, w_up, w_down):
    tok_count, model_width = tokens.shape
    route_count = expert_ids.shape[1]
    expert_ranks = lax.axis_size("expert")
    local_experts = w_gate.shape[0]
    experts = local_experts * expert_ranks
    capacity = 3 * tok_count * route_count // (2 * experts)
    routes = tok_count * route_count
    total_slots = experts * capacity
    flat_ids = expert_ids.reshape(routes)
    one_hot = (flat_ids[:, None] == jnp.arange(experts, dtype=jnp.int32)[None, :]).astype(jnp.int32)
    slot_order = jnp.sum((jnp.cumsum(one_hot, axis=0) - 1) * one_hot, axis=1)
    local_index = flat_ids % local_experts
    owner_rank = flat_ids // local_experts
    destination = (local_index * expert_ranks + owner_rank) * capacity + slot_order
    source = (
        jnp.full((total_slots,), routes, jnp.int32)
        .at[destination]
        .set(jnp.arange(routes, dtype=jnp.int32))
    )
    filled = source < routes
    from_route = jnp.minimum(source, routes - 1)
    from_token = from_route // route_count
    zero_value = jnp.zeros((), jnp.bfloat16)
    send_tokens = jnp.where(filled[:, None], tokens[from_token], zero_value).reshape(
        local_experts, expert_ranks * capacity, model_width
    )
    send_grads = jnp.where(filled[:, None], out_grad[from_token], zero_value).reshape(
        local_experts, expert_ranks * capacity, model_width
    )
    send_weights = jnp.where(filled, route_weight.reshape(routes)[from_route], zero_value).reshape(
        local_experts, expert_ranks * capacity
    )
    recv_weights = lax.all_to_all(send_weights, "expert", split_axis=1, concat_axis=1, tiled=True)
    recv_tokens, recv_grads = side_by_side((send_tokens, send_grads), "expert", 1, 1, 0)
    full_gate, full_up = sent_together((w_gate, w_up), "dp", 1, 0)
    full_down = lax.all_gather(w_down, "dp", axis=2, tiled=True)
    gate_value = jnp.einsum(
        "erd,edf->erf", recv_tokens, full_gate, preferred_element_type=jnp.float32
    )
    up_value = jnp.einsum("erd,edf->erf", recv_tokens, full_up, preferred_element_type=jnp.float32)
    sigmoid_gate = jax.nn.sigmoid(gate_value)
    activated = gate_value * sigmoid_gate
    hidden = (activated * up_value).astype(jnp.bfloat16)
    scaled = (recv_weights.astype(jnp.float32)[:, :, None] * recv_grads).astype(jnp.bfloat16)
    expert_out = jnp.einsum("erf,efd->erd", hidden, full_down, preferred_element_type=jnp.float32)
    route_dot = jnp.sum(expert_out * recv_grads, axis=2)
    hidden_grad = jnp.einsum("erd,efd->erf", scaled, full_down, preferred_element_type=jnp.float32)
    down_term = jnp.einsum("erf,erd->efd", hidden, scaled, preferred_element_type=jnp.float32)
    gate_delta = (
        hidden_grad * up_value * sigmoid_gate * (1.0 + gate_value * (1.0 - sigmoid_gate))
    ).astype(jnp.bfloat16)
    up_delta = (hidden_grad * activated).astype(jnp.bfloat16)
    input_grad = (
        jnp.einsum("erf,edf->erd", gate_delta, full_gate, preferred_element_type=jnp.float32)
        + jnp.einsum("erf,edf->erd", up_delta, full_up, preferred_element_type=jnp.float32)
    ).astype(jnp.bfloat16)
    back_dots = lax.all_to_all(
        route_dot.astype(jnp.bfloat16), "expert", split_axis=1, concat_axis=1, tiled=True
    )
    back_rows = lax.all_to_all(input_grad, "expert", split_axis=1, concat_axis=1, tiled=True)
    gate_term = jnp.einsum(
        "erd,erf->edf", recv_tokens, gate_delta, preferred_element_type=jnp.float32
    )
    up_term = jnp.einsum("erd,erf->edf", recv_tokens, up_delta, preferred_element_type=jnp.float32)
    gate_sum, up_sum, down_sum = (
        *tuple(
            (
                part.astype(jnp.float32)
                for part in side_by_side_2(
                    (gate_term.astype(jnp.bfloat16), up_term.astype(jnp.bfloat16)), "dp", 1, 0
                )
            )
        ),
        lax.psum_scatter(
            down_term.astype(jnp.bfloat16), "dp", scatter_dimension=2, tiled=True
        ).astype(jnp.float32),
    )
    down_grad = down_sum.astype(jnp.bfloat16)
    gate_grad = gate_sum.astype(jnp.bfloat16)
    up_grad = up_sum.astype(jnp.bfloat16)
    route_rows = back_rows.reshape(total_slots, model_width)[destination]
    token_grad = jnp.sum(
        route_rows.astype(jnp.float32).reshape(tok_count, route_count, model_width), axis=1
    ).astype(jnp.bfloat16)
    route_grad = back_dots.reshape(total_slots)[destination].reshape(tok_count, route_count)
    return (token_grad, route_grad, gate_grad, up_grad, down_grad)


def solution(mesh):
    placed = (
        P(("dp", "expert"), None),
        P(("dp", "expert"), None),
        P(("dp", "expert"), None),
        P(("dp", "expert"), None),
        P("expert", "dp", None),
        P("expert", "dp", None),
        P("expert", None, "dp"),
    )
    return jax.shard_map(
        on_device,
        mesh=mesh,
        in_specs=placed,
        out_specs=(
            P(("dp", "expert"), None),
            P(("dp", "expert"), None),
            P("expert", "dp", None),
            P("expert", "dp", None),
            P("expert", None, "dp"),
        ),
        check_vma=False,
    )
```

profile of v0, /device:TPU:1, one launch (start us, length us, event | category | flops | bytes accessed | tf_op | source)
XLA Modules:
  0.0 557.5 jit_solution(7284041077687638340)
XLA Ops:
  7.2 0.0 all-gather.3.cloned.1.call-start
  7.2 0.7 all-gather.3.cloned.1.call-update
  7.9 0.8 copy.28
  8.8 0.1 eq.31
  8.9 0.1 eq.27
  9.0 0.8 copy.31
  9.9 0.2 reshape.222
  10.0 0.7 broadcast_multiply_fusion
  10.7 0.1 copy.27
  10.9 0.1 mul.64
  11.0 1.4 reduce-window.6
  12.5 0.2 slice_reduce_fusion
  12.8 0.1 fusion.17
  12.9 4.1 scatter_custom_fusion
  17.0 6.5 %gather_fusion = bf16[960]{0:T(1024)(128)(2,1)S(1)} fusion(bf16[640]{0:T(1024)(128)(2,1)S(1)} %reshape.222, s32[1024]{0:T(1024)S(1)} %get-tuple-element.34), kind=kCustom, calls=%fused_computation | custom fusion | bytes 7680 | tf_op jit(solution)/shard_map/gather | solution.py:62
  23.5 0.7 all_to_all.21
  24.2 9.3 %all-to-all-start = ((bf16[1,16,60]{2,0,1:T(2,128)(2,1)}), bf16[1,16,60]{2,0,1:T(2,128)(2,1)S(1)}, u32[]{:S(2)}, u32[]{:S(2)}) async-start(bf16[1,16,60]{2,0,1:T(2,128)(2,1)} %all_to_all.21), calls=%async_computation | async-start | bytes 16384 | tf_op jit(solution)/shard_map/all_to_all | solution.py:65
  33.5 0.0 all-gather.5.cloned.1.call-start
  33.5 0.9 pad_maximum_fusion.2
  34.5 0.0 all-gather.5.cloned.1.call-update
  34.5 5.9 %gather_fusion.2 = bf16[960,2048]{1,0:T(8,128)(2,1)} fusion(bf16[320,2048]{1,0:T(8,128)(2,1)S(1)} %copy-done, s32[1024]{0:T(1024)S(1)} %get-tuple-element.33), kind=kCustom, calls=%fused_computation.2 | custom fusion | bytes 7868160 | tf_op jit(solution)/shard_map/gather | solution.py:59
  40.5 5.9 %gather_fusion.1 = bf16[960,2048]{1,0:T(8,128)(2,1)} fusion(bf16[320,2048]{1,0:T(8,128)(2,1)S(1)} %copy-done.2, s32[1024]{0:T(1024)S(1)} %get-tuple-element.33), kind=kCustom, calls=%fused_computation.1 | custom fusion | bytes 7868160 | tf_op jit(solution)/shard_map/gather | solution.py:56
  46.4 5.7 %bitcast_select_fusion.1 = (bf16[1,960,2048]{2,1,0:T(8,128)(2,1)}, bf16[1,960,2048]{2,1,0:T(8,128)(2,1)}) fusion(bf16[960,2048]{1,0:T(8,128)(2,1)} %gather_fusion.1, pred[960]{0:T(1024)(128)(4,1)S(1)} %get-tuple-element.21, bf16[960,2048]{1,0:T(8,128)(2,1)} %gather_fusion.2), kind=kLoop, calls=%fused_computation.18 | loop fusion | flops 3932160 | bytes 15729600 | tf_op jit(solution)/shard_map/jit(_where)/select_n | solution.py:56
  52.1 4.0 pad_maximum_fusion
  56.1 23.4 %copy.33 = bf16[2,960,2048]{2,0,1:T(2,128)(2,1)} copy(bf16[2,960,2048]{2,1,0:T(8,128)(2,1)S(1)} %pad_maximum_fusion) | data formatting | bytes 15728640 | tf_op jit(solution)/shard_map/concatenate | solution.py:9
  79.5 7.2 %all-to-all-start.1 = ((bf16[2,960,2048]{2,0,1:T(2,128)(2,1)}), bf16[2,960,2048]{2,0,1:T(2,128)(2,1)}, u32[]{:S(2)}, u32[]{:S(2)}) async-start(bf16[2,960,2048]{2,0,1:T(2,128)(2,1)} %copy.33), calls=%async_computation.1 | async-start | bytes 15728640 | tf_op jit(solution)/shard_map/all_to_all | solution.py:10
  86.7 0.6 reduce-scatter.3.cloned.1.call-start
  87.3 0.1 reshape.231
  87.4 165.9 %all-to-all-done.1 = bf16[2,960,2048]{2,0,1:T(2,128)(2,1)} async-done(((bf16[2,960,2048]{2,0,1:T(2,128)(2,1)}), bf16[2,960,2048]{2,0,1:T(2,128)(2,1)}, u32[]{:S(2)}, u32[]{:S(2)}) %all-to-all-start.1) | async-done | bytes 7864352 | tf_op jit(solution)/shard_map/all_to_all | solution.py:10
  253.3 16.2 %fusion.26 = (bf16[1,960,2048]{2,0,1:T(2,128)(2,1)}, bf16[1,960,2048]{2,0,1:T(2,128)(2,1)S(1)}) fusion(bf16[2,960,2048]{2,0,1:T(2,128)(2,1)} %all-to-all-done.1), kind=kLoop, calls=%fused_computation.69 | loop fusion | bytes 15728640 | tf_op jit(solution)/shard_map/split | solution.py:11
  269.4 4.5 copy.56
  273.9 10.5 %fusion.5 = f32[960,768]{1,0:T(8,128)} fusion(bf16[1,768,2048]{2,1,0:T(8,128)(2,1)} %all-gather.3.cloned.1.call-done, f32[960]{0:T(1024)S(1)} %reshape.231, bf16[1,960,2048]{2,0,1:T(2,128)(2,1)} %get-tuple-element.22), kind=kOutput, calls=%fused_computation.25 | convolution fusion | flops 3025797120 | bytes 10030848 | tf_op jit(solution)/shard_map/erd,efd->erf/dot_general | solution.py:79
  284.4 7.1 %all-gather.5.cloned.1.call-done = bf16[2,2048,768]{2,1,0:T(8,128)(2,1)} async-done(((bf16[2,256,768]{2,1,0:T(8,128)(2,1)}), bf16[2,2048,768]{2,1,0:T(8,128)(2,1)}) %all-gather.5.cloned.1.call-update) | async-done | bytes 6291472 | tf_op jit(solution)/shard_map/all_gather | solution.py:16
  291.5 6.4 %fusion.13 = f32[960,768]{1,0:T(8,128)S(1)} fusion(bf16[960,2048]{1,0:T(8,128)(2,1)} %bitcast.73, bf16[2,2048,768]{2,1,0:T(8,128)(2,1)} %all-gather.5.cloned.1.call-done), kind=kOutput, calls=%fused_computation.37 | convolution fusion | flops 3019898880 | bytes 10027008 | tf_op jit(solution)/shard_map/erd,edf->erf/dot_general | solution.py:69
  298.0 0.4 copy-done.7
  298.4 5.2 multiply_convert_fusion
  303.6 4.0 fusion.7
  307.6 3.8 fusion.8
  311.4 3.2 pad_maximum_fusion.1
  314.7 0.0 reduce-scatter.3.cloned.1.call-update
  314.7 0.0 reduce-scatter.5.cloned.1.call-start
  314.8 10.7 %fusion.9 = bf16[1,768,2048]{2,1,0:T(8,128)(2,1)} fusion(bf16[960,768]{1,0:T(8,128)(2,1)} %get-tuple-element.24, f32[960]{0:T(1024)S(1)} %reshape.231, bf16[1,960,2048]{2,0,1:T(2,128)(2,1)} %get-tuple-element.22), kind=kOutput, calls=%fused_computation.29 | convolution fusion | flops 3027369984 | bytes 8556288 | tf_op jit(solution)/shard_map/erf,erd->efd/dot_general | solution.py:80
  325.5 9.3 %fusion.1 = bf16[960]{0:T(1024)(128)(2,1)S(1)} fusion(bf16[960,768]{1,0:T(8,128)(2,1)} %get-tuple-element.24, bf16[1,768,2048]{2,1,0:T(8,128)(2,1)} %all-gather.3.cloned.1.call-done, bf16[1,960,2048]{2,0,1:T(2,128)(2,1)} %get-tuple-element.22), kind=kOutput, calls=%fused_computation.9 | convolution fusion | flops 3025796096 | bytes 8554368 | tf_op jit(solution)/shard_map/erf,efd->erd/dot_general | solution.py:77
  334.8 0.7 convert_element_type.103
  335.5 8.2 %all-to-all-start.3 = ((bf16[1,16,60]{2,0,1:T(2,128)(2,1)}), bf16[1,16,60]{2,0,1:T(2,128)(2,1)S(1)}, u32[]{:S(2)}, u32[]{:S(2)}) async-start(bf16[1,16,60]{2,0,1:T(2,128)(2,1)} %convert_element_type.103), calls=%async_computation.3 | async-start | bytes 16384 | tf_op jit(solution)/shard_map/all_to_all | solution.py:89
  343.7 5.2 fusion.12
  349.0 5.4 fusion.2
  354.4 23.1 %copy.58 = bf16[1,960,2048]{2,0,1:T(2,128)(2,1)} copy(bf16[1,960,2048]{2,1,0:T(8,128)(2,1)S(1)} %fusion.2) | data formatting | bytes 7864320 | tf_op jit(solution)/shard_map/convert_element_type | solution.py:88
  377.5 0.5 broadcast.192
  378.0 25.2 %reduce.11 = bf16[960,2048]{1,0:T(8,128)(2,1)} reduce(bf16[960,1,2048]{2,1,0:T(2,128)(2,1)} %bitcast.71, bf16[]{:T(256)} %broadcast.192), dimensions={1}, to_apply=%bitcast.67.reduce_sub_computation | reduce | bytes 7864322
  403.2 8.9 %reshape.295 = bf16[16,2,61440]{2,1,0:T(2,128)(2,1)} reshape(bf16[960,2048]{1,0:T(8,128)(2,1)} %reduce.11) | data formatting | bytes 7864320
  412.1 7.6 %all-to-all-start.2 = ((bf16[16,2,61440]{2,1,0:T(2,128)(2,1)}), bf16[16,2,61440]{2,1,0:T(2,128)(2,1)}, u32[]{:S(2)}, u32[]{:S(2)}) async-start(bf16[16,2,61440]{2,1,0:T(2,128)(2,1)} %reshape.295), calls=%async_computation.2 | async-start | bytes 7864320 | tf_op jit(solution)/shard_map/all_to_all | solution.py:92
  419.7 0.1 reshape.229
  419.8 4.3 gather_fusion.4
  424.1 0.2 reshape.230
  424.3 0.7 copy.38
  425.0 69.0 %all-to-all-done.2 = bf16[16,2,61440]{2,1,0:T(2,128)(2,1)} async-done(((bf16[16,2,61440]{2,1,0:T(2,128)(2,1)}), bf16[16,2,61440]{2,1,0:T(2,128)(2,1)}, u32[]{:S(2)}, u32[]{:S(2)}) %all-to-all-start.2) | async-done | bytes 3932192 | tf_op jit(solution)/shard_map/all_to_all | solution.py:92
  494.0 12.2 %reshape.296 = bf16[960,1,2048]{2,1,0:T(2,128)(2,1)} reshape(bf16[16,2,61440]{2,1,0:T(2,128)(2,1)} %all-to-all-done.2) | data formatting | bytes 7864320
  506.3 7.6 %copy.57 = bf16[1,960,2048]{2,1,0:T(8,128)(2,1)} copy(bf16[1,960,2048]{2,0,1:T(2,128)(2,1)} %bitcast.72) | data formatting | bytes 7864320
  513.9 9.6 %gather_fusion.3 = bf16[640,2048]{1,0:T(8,128)(2,1)} fusion(bf16[960,2048]{1,0:T(8,128)(2,1)} %bitcast.70, s32[1024]{0:T(1024)S(1)} %pad_clamp_fusion), kind=kCustom, calls=%fused_computation.3 | custom fusion | bytes 5245440 | tf_op jit(solution)/shard_map/gather | solution.py:113
  523.5 5.7 %gather.27 = bf16[320,2,2048]{2,1,0:T(2,128)(2,1)} reshape(bf16[640,2048]{1,0:T(8,128)(2,1)} %gather_fusion.3) | data formatting | bytes 5242880 | tf_op jit(solution)/shard_map/gather | solution.py:113
  529.2 9.2 %reduce_sum.34 = bf16[320,2048]{1,0:T(8,128)(2,1)} reduce(bf16[320,2,2048]{2,1,0:T(2,128)(2,1)} %gather.27, bf16[]{:T(256)} %constant.58.clone.1), dimensions={1}, to_apply=%region_4.5 | reduce | flops 655360 | bytes 3932162 | tf_op jit(solution)/shard_map/reduce_sum | solution.py:114
  538.4 2.0 fusion.27
  540.4 10.0 %reduce-scatter.5.cloned.1.call-done = bf16[1,768,256]{2,1,0:T(8,128)(2,1)} async-done(((bf16[1,768,2048]{2,1,0:T(8,128)(2,1)}), bf16[1,768,256]{2,1,0:T(8,128)(2,1)}) %reduce-scatter.5.cloned.1.call-update) | async-done | bytes 393232 | tf_op jit(solution)/shard_map/reduce_scatter | solution.py:106
  (34 shorter events, 0.2 us)
Async XLA Ops:
  7.2 27.4 %copy-start = (bf16[320,2048]{1,0:T(8,128)(2,1)S(1)}, bf16[320,2048]{1,0:T(8,128)(2,1)}, u32[]{:S(2)}) copy-start(bf16[320,2048]{1,0:T(8,128)(2,1)} %param.8) | copy-start | bytes 3932164
  7.2 26.3 %copy-start.4 = (bf16[1,256,768]{2,1,0:T(8,128)(2,1)S(1)}, bf16[1,256,768]{2,1,0:T(8,128)(2,1)}, u32[]{:S(2)}) copy-start(bf16[1,256,768]{2,1,0:T(8,128)(2,1)} %param.12) | copy-start | bytes 1179652
  7.2 26.3 %copy-start.5 = (bf16[1,256,768]{2,1,0:T(8,128)(2,1)S(1)}, bf16[1,256,768]{2,1,0:T(8,128)(2,1)}, u32[]{:S(2)}) copy-start(bf16[1,256,768]{2,1,0:T(8,128)(2,1)} %param.11) | copy-start | bytes 1179652
  7.2 266.7 %all-gather.3.cloned.1.call-start = ((), (), s32[]{:S(2)}) async-start(), calls=%async_computation.6 | async-start | bytes 3538944 | tf_op jit(solution)/shard_map/all_gather | solution.py:68
  24.2 55.3 %all-to-all-start = ((bf16[1,16,60]{2,0,1:T(2,128)(2,1)}), bf16[1,16,60]{2,0,1:T(2,128)(2,1)S(1)}, u32[]{:S(2)}, u32[]{:S(2)}) async-start(bf16[1,16,60]{2,0,1:T(2,128)(2,1)} %all_to_all.21), calls=%async_computation | async-start | bytes 16384 | tf_op jit(solution)/shard_map/all_to_all | solution.py:65
  33.5 258.0 %all-gather.5.cloned.1.call-start = ((), (), s32[]{:S(2)}) async-start(), calls=%async_computation.7 | async-start | bytes 7077888 | tf_op jit(solution)/shard_map/all_gather | solution.py:16
  34.5 5.9 %copy-start.2 = (bf16[320,2048]{1,0:T(8,128)(2,1)S(1)}, bf16[320,2048]{1,0:T(8,128)(2,1)}, u32[]{:S(2)}) copy-start(bf16[320,2048]{1,0:T(8,128)(2,1)} %param.7) | copy-start | bytes 3932164
  79.5 173.8 %all-to-all-start.1 = ((bf16[2,960,2048]{2,0,1:T(2,128)(2,1)}), bf16[2,960,2048]{2,0,1:T(2,128)(2,1)}, u32[]{:S(2)}, u32[]{:S(2)}) async-start(bf16[2,960,2048]{2,0,1:T(2,128)(2,1)} %copy.33), calls=%async_computation.1 | async-start | bytes 15728640 | tf_op jit(solution)/shard_map/all_to_all | solution.py:10
  86.7 451.7 %reduce-scatter.3.cloned.1.call-start = ((), (), s32[]{:S(2)}) async-start(), calls=%async_computation.8 | async-start | bytes 7077888 | tf_op jit(solution)/shard_map/reduce_scatter | solution.py:25
  291.5 6.4 %copy-start.3 = (bf16[1,960,2048]{2,1,0:T(8,128)(2,1)S(1)}, bf16[1,960,2048]{2,1,0:T(8,128)(2,1)}, u32[]{:S(2)}) copy-start(bf16[1,960,2048]{2,1,0:T(8,128)(2,1)} %copy.56) | copy-start | bytes 11796484
  291.5 6.4 %copy-start.6 = (bf16[2,2048,768]{2,1,0:T(8,128)(2,1)S(1)}, bf16[2,2048,768]{2,1,0:T(8,128)(2,1)}, u32[]{:S(2)}) copy-start(bf16[2,2048,768]{2,1,0:T(8,128)(2,1)} %all-gather.5.cloned.1.call-done) | copy-start | bytes 18874372
  291.5 6.9 %copy-start.7 = (f32[960,768]{1,0:T(8,128)S(1)}, f32[960,768]{1,0:T(8,128)}, u32[]{:S(2)}) copy-start(f32[960,768]{1,0:T(8,128)} %fusion.5) | copy-start | bytes 8847364
  303.6 4.0 copy-start.8
  314.7 235.8 %reduce-scatter.5.cloned.1.call-start = ((), (), s32[]{:S(2)}) async-start(), calls=%async_computation.9 | async-start | bytes 3538944 | tf_op jit(solution)/shard_map/reduce_scatter | solution.py:106
  335.5 76.6 %all-to-all-start.3 = ((bf16[1,16,60]{2,0,1:T(2,128)(2,1)}), bf16[1,16,60]{2,0,1:T(2,128)(2,1)S(1)}, u32[]{:S(2)}, u32[]{:S(2)}) async-start(bf16[1,16,60]{2,0,1:T(2,128)(2,1)} %convert_element_type.103), calls=%async_computation.3 | async-start | bytes 16384 | tf_op jit(solution)/shard_map/all_to_all | solution.py:89
  343.7 5.3 copy-start.9
  412.1 81.9 %all-to-all-start.2 = ((bf16[16,2,61440]{2,1,0:T(2,128)(2,1)}), bf16[16,2,61440]{2,1,0:T(2,128)(2,1)}, u32[]{:S(2)}, u32[]{:S(2)}) async-start(bf16[16,2,61440]{2,1,0:T(2,128)(2,1)} %reshape.295), calls=%async_computation.2 | async-start | bytes 7864320 | tf_op jit(solution)/shard_map/all_to_all | solution.py:92
  523.5 27.0 %copy-start.1 = (bf16[320,2048]{1,0:T(8,128)(2,1)S(1)}, bf16[320,2048]{1,0:T(8,128)(2,1)}, u32[]{:S(2)}) copy-start(bf16[320,2048]{1,0:T(8,128)(2,1)} %param.8) | copy-start | bytes 3932164
Sparse Core Ops, SparseCore 0:
  9.6 72.8 all-gather.2
  84.7 206.7 all-gather.4
  314.8 154.5 reduce-scatter.2
  472.3 78.1 reduce-scatter.4
where the time goes:
time: 564 us; the launch traced here: 558 us
  waiting for transfers between devices  253 us (45%)
  local copies, waits for them, and re-layouts  146 us (26%)
  matrix products  60.6 us (11%)
  other arithmetic  50.7 us (9%)
  starting transfers between devices  33 us (6%)
  between operations  14.6 us (3%)
    all_to_all x1, waiting for transfers between devices, side_by_side(): lax.all_to_all(both, axis, split_axis=split_dim, concat_axis=concat_dim,...  166 us
    all_to_all x1, waiting for transfers between devices, on_device(): lax.all_to_all(input_grad, 'expert', split_axis=1, concat_axis=1, tiled=T...  69 us
    unnamed x28, local copies, waits for them, and re-layouts  36.5 us
    unnamed x1, other arithmetic  25.2 us
    concatenate x1, local copies, waits for them, and re-layouts, side_by_side(): both = jnp.concatenate(arrays, axis=along)  23.4 us
    convert_element_type x1, local copies, waits for them, and re-layouts, on_device(): input_grad = (jnp.einsum('erf,edf->erd', gate_delta, full_gate, preferred...  23.1 us
    split x1, local copies, waits for them, and re-layouts, side_by_side(): jnp.split(out, [sum(widths[:k]) for k in range(1, len(widths))], axis=along)  16.2 us
    gather x2, local copies, waits for them, and re-layouts, on_device(): route_rows = back_rows.reshape(total_slots, model_width)[destination]  15.3 us
  transfers between devices with their start and end apart: 8, of which 4 were waited for; matrix products, arithmetic and copies ran while one was open for 42% of the time, Pallas kernels for 0%

commit v1 on v0

v1 whole, which is shorter than its diff:
```python
import jax
import jax.numpy as jnp
from jax import lax
from jax.experimental import pallas as pl
from jax.experimental.pallas import tpu as pltpu
from jax.sharding import PartitionSpec as P

MESH = pl.DeviceIdType.MESH
F32 = jnp.float32
BF16 = jnp.bfloat16
T = 320
D = 2048
FF = 768
CH = 256
NCH = 8
CAP = 60
RB = 128
RV = 2 * CAP
NB = 8
ROWS = NB * RB


def nn(a, b):
    return jnp.dot(a, b, preferred_element_type=F32)


def nt(a, b):
    return lax.dot_general(a, b, (((1,), (1,)), ((), ())), preferred_element_type=F32)


def tn(a, b):
    return lax.dot_general(a, b, (((0,), (0,)), ((), ())), preferred_element_type=F32)


def rem(a, b):
    return lax.rem(a, jnp.int32(b))


def quo(a, b):
    return lax.div(a, jnp.int32(b))


def device(x, y, z, c):
    x, y, z, c = rem(x + 4, 4), rem(y + 4, 4), rem(z + 4, 4), rem(c + 2, 2)
    return {"dp": y * 2 + rem(x, 2), "expert": quo(x, 2) * 8 + z * 2 + c}


def kernel(
    tokens_hbm, grads_hbm, ids_hbm, rw_hbm, wg_hbm, wu_hbm, wd_hbm,
    token_out, route_out, gate_out, up_out, down_out,
    tk, og, ids, rw, meta, xmeta, xr, slots, go, gp, gto, gtp,
    zs, zr, zms, zmr, wg, wu, wd, gd, ud, hwt,
    rag, rau, rad, rbg, rbu, rbd, rxg, rxu, rxd,
    ret, zds, rdot, pown, xr2, ddown, dpar, xdot,
    lsem, osem, xss, xrs, zss, zrs, ags, agr, zts, ztr, xts, xtr,
    ras, rar, rbs, rbr, rxs, rxr,
):
    dp, ex = lax.axis_index("dp"), lax.axis_index("expert")
    x_lo, y = rem(dp, 2), quo(dp, 2)
    x_hi, z, c = quo(ex, 8), rem(quo(ex, 2), 4), rem(ex, 2)
    x = x_hi * 2 + x_lo
    me = z * 2 + c
    xfar = device(x + 2, y, z, c)
    xnear = {"dp": y * 2 + 1 - x_lo, "expert": ex}
    yup, ydn = device(x, y + 1, z, c), device(x, y - 1, z, c)
    ydir = (yup, ydn)

    def peer(b):
        return {"dp": dp, "expert": x_hi * 8 + b}

    def put(src, dst, ss, rs, to):
        return pltpu.make_async_remote_copy(
            src_ref=src, dst_ref=dst, send_sem=ss, recv_sem=rs, device_id=to, device_id_type=MESH
        )

    def got(dst, rs):
        put(dst, dst, rs, rs, xfar).wait_recv()

    def sent(src, ss):
        put(src, src, ss, ss, xfar).wait_send()

    def chunk_col(j):
        k, l = rem(j, 4), quo(j, 4)
        dy = k + quo(k, 2) * (1 - 2 * rem(k, 2))
        owner = 2 * rem(y + dy, 4) + rem(x_lo + l, 2)
        return pl.multiple_of(owner * CH, CH)

    loads = [
        pltpu.make_async_copy(s, d, lsem.at[n])
        for n, (s, d) in enumerate(
            (
                (ids_hbm, ids), (rw_hbm, rw), (tokens_hbm, tk), (grads_hbm, og),
                (wg_hbm, wg.at[0]), (wu_hbm, wu.at[0]), (wd_hbm, wd.at[0]),
            )
        )
    ]
    for cp in loads:
        cp.start()

    def clear(j, _):
        zr[j, :, RV:, :] = jnp.zeros((NB, RB - RV, 2 * CH), BF16)
        ret[j, :, RV:, :] = jnp.zeros((NB, RB - RV, CH), BF16)
        return 0

    lax.fori_loop(0, NCH, clear, 0)
    zmr[:, RV:, :] = jnp.zeros((NB, RB - RV, 128), BF16)
    rdot[:, RV:, :] = jnp.zeros((NB, RB - RV, 128), BF16)

    barrier = pltpu.get_barrier_semaphore()
    greet = [xfar, xnear, yup, ydn] + [peer(rem(me + r, NB)) for r in range(1, NB)]
    for d in greet:
        pl.semaphore_signal(barrier, inc=1, device_id=d, device_id_type=MESH)
    for cp in loads:
        cp.wait()

    lane = lax.broadcasted_iota(jnp.int32, (T, 128), 1)
    id0, id1 = ids[:, 0:1], ids[:, 1:2]
    w0, w1 = rw[:, 0:1].astype(F32), rw[:, 1:2].astype(F32)
    weight_of = jnp.where(lane == id0, w0, 0.0) + jnp.where(lane == id1, w1, 0.0)
    named = jnp.where((lane - 16 == id0) | (lane - 16 == id1), 1.0, 0.0)
    meta[...] = (weight_of + named).astype(BF16)

    pl.semaphore_wait(barrier, len(greet))

    put(meta, xmeta, xss.at[NCH, 0], xrs.at[NCH, 0], xfar).start()

    def xchunk(j):
        col = chunk_col(jnp.int32(j))
        put(tk.at[:, pl.ds(col, CH)], xr.at[j, :, pl.ds(0, CH)], xss.at[j, 0], xrs.at[j, 0], xfar).start()
        put(og.at[:, pl.ds(col, CH)], xr.at[j, :, pl.ds(CH, CH)], xss.at[j, 1], xrs.at[j, 1], xfar).start()

    w_all = (wg, wu, wd)

    def shard(n, src, dst, to):
        put(w_all[n].at[src], w_all[n].at[dst], ags.at[dst, n, 0], agr.at[dst, n, 0], to).start()

    def half(n, src, dst, h, to):
        size = w_all[n].shape[1] // 2
        rows = pl.ds(h * size, size)
        put(
            w_all[n].at[src, rows], w_all[n].at[dst, rows], ags.at[dst, n, h], agr.at[dst, n, h], to
        ).start()

    for n in range(3):
        shard(n, 0, 2, yup)
        shard(n, 0, 1, ydn)
    xchunk(0)
    xchunk(1)
    shard(0, 0, 4, xnear)
    xchunk(2)
    shard(1, 0, 4, xnear)
    xchunk(3)
    shard(2, 0, 4, xnear)
    for j in range(4, NCH):
        xchunk(j)

    before = (
        lax.broadcasted_iota(jnp.int32, (T, T), 0) < lax.broadcasted_iota(jnp.int32, (T, T), 1)
    ).astype(BF16)
    same = (
        lax.broadcasted_iota(jnp.int32, (T, T), 0) == lax.broadcasted_iota(jnp.int32, (T, T), 1)
    ).astype(BF16)

    def tables(src, first, g, gt, which):
        table = src[...]
        listed, rank = tn(table, same), tn(table, before)
        slots[which] = jnp.where(listed > 0.5, rank + first, -1.0)
        slot_id = lax.broadcasted_iota(jnp.int32, (RB, T), 0).astype(F32)

        def one(b, _):
            row = slots[which, pl.ds(16 + x_hi * 8 + b, 1), :]
            hot = jnp.where(slot_id == row, 1.0, 0.0)
            g[b] = hot.astype(BF16)
            gt[:, pl.ds(pl.multiple_of(b * RB, RB), RB)] = hot.T.astype(BF16)
            return 0

        lax.fori_loop(0, NB, one, 0)

    tables(meta, 0.0, go, gto, 0)
    got(xmeta, xrs.at[NCH, 0])
    tables(xmeta, float(CAP), gp, gtp, 1)

    rows_sent = pl.ds(0, RV)

    def to_peers(start, own, zz):
        for cc in range(2):
            b = zz * 2 + cc

            @pl.when(b != me)
            def _():
                start(b)

            @pl.when(b == me)
            def _():
                own(b)

    def weights_table(m, _):
        zz = rem(z + 1 + m, 4)
        two = pl.ds(zz * 2, 2)
        picked = nn(go[two].reshape(2 * RB, T), meta[...]) + nn(
            gp[two].reshape(2 * RB, T), xmeta[...]
        )
        zms[two] = picked.astype(BF16).reshape(2, RB, 128)

        def start(b):
            put(
                zms.at[b, rows_sent], zmr.at[me, rows_sent], zss.at[NCH], zrs.at[NCH], peer(b)
            ).start()

        def own(b):
            zmr[b] = zms[b]

        to_peers(start, own, zz)
        return 0

    lax.fori_loop(0, 4, weights_table, 0)

    seven = pl.ds(0, NB - 1)

    def forward_phase(ag, au, ah):
        def reset(m, _):
            rows = pl.ds(pl.multiple_of(m * RB, RB), RB)
            ag[rows] = jnp.zeros((RB, FF), F32)
            au[rows] = jnp.zeros((RB, FF), F32)
            ah[rows] = jnp.zeros((RB, FF), F32)
            return 0

        lax.fori_loop(0, NB, reset, 0)

        def produce(j):
            slot = rem(j, 2)
            col = chunk_col(j)
            got(xr.at[j, :, pl.ds(0, CH)], xrs.at[j, 0])
            got(xr.at[j, :, pl.ds(CH, CH)], xrs.at[j, 1])

            @pl.when(j >= 2)
            def _():
                sent(zs.at[slot, seven, rows_sent], zss.at[j - 2])

            def gather(m, _):
                zz = rem(z + 1 + m, 4)
                two = pl.ds(zz * 2, 2)
                mine, theirs = go[two].reshape(2 * RB, T), gp[two].reshape(2 * RB, T)
                rows_t = nn(mine, tk[:, pl.ds(col, CH)]) + nn(theirs, xr[j, :, :CH])
                zs[slot, two, :, :CH] = rows_t.astype(BF16).reshape(2, RB, CH)
                rows_g = nn(mine, og[:, pl.ds(col, CH)]) + nn(theirs, xr[j, :, CH:])
                zs[slot, two, :, CH:] = rows_g.astype(BF16).reshape(2, RB, CH)

                def start(b):
                    put(
                        zs.at[slot, b, rows_sent], zr.at[j, me, rows_sent],
                        zss.at[j], zrs.at[j], peer(b),
                    ).start()

                def own(b):
                    zr[j, b] = zs[slot, b]

                to_peers(start, own, zz)
                return 0

            lax.fori_loop(0, 4, gather, 0)

        def got_shard(idx):
            for n in range(3):
                got(w_all[n].at[idx], agr.at[idx, n, 0])

        def got_halves(idx):
            for n in range(3):
                size = w_all[n].shape[1] // 2
                for h in range(2):
                    got(w_all[n].at[idx, pl.ds(h * size, size)], agr.at[idx, n, h])

        def consume(j):
            @pl.when(j == 1)
            def _():
                got_shard(1)
                got_shard(2)
                for n in range(3):
                    half(n, 1, 3, 1, ydn)
                    half(n, 2, 3, 0, yup)

            @pl.when(j == 3)
            def _():
                got_halves(3)
                got_shard(4)
                for n in range(3):
                    shard(n, 4, 6, yup)
                    shard(n, 4, 5, ydn)

            @pl.when(j == 5)
            def _():
                got_shard(5)
                got_shard(6)
                for n in range(3):
                    half(n, 5, 7, 1, ydn)
                    half(n, 6, 7, 0, yup)

            @pl.when(j == 7)
            def _():
                got_halves(7)

            got(zr.at[j, seven, rows_sent], zrs.at[j])

            def tile(m, _):
                block = zr[j, pl.ds(m * 2, 2)].reshape(2 * RB, 2 * CH)
                rows = pl.ds(pl.multiple_of(m * 2 * RB, 2 * RB), 2 * RB)
                ag[rows] += nn(block[:, :CH], wg[j])
                au[rows] += nn(block[:, :CH], wu[j])
                ah[rows] += nt(block[:, CH:], wd[j])
                return 0

            lax.fori_loop(0, 4, tile, 0)

        def step(j, _):
            @pl.when(j < NCH)
            def _():
                produce(j)

            @pl.when(j > 0)
            def _():
                consume(j - 1)

            return 0

        lax.fori_loop(0, NCH + 1, step, 0)

        got(zmr.at[seven, rows_sent], zrs.at[NCH])
        lane_of = lax.broadcasted_iota(jnp.int32, (RB, 128), 1)

        def delta(b, _):
            rows = pl.ds(pl.multiple_of(b * RB, RB), RB)
            weight = jnp.sum(
                jnp.where(lane_of == ex, zmr[b].astype(F32), 0.0), axis=1, keepdims=True
            )
            gate, up, back = ag[rows], au[rows], ah[rows]
            sig = jax.nn.sigmoid(gate)
            act = gate * sig
            hidden = (act * up).astype(BF16).astype(F32)
            dot = jnp.sum(hidden * back, axis=1, keepdims=True)
            zds[b] = jnp.where(lane_of == ex, dot, 0.0).astype(BF16)
            back = back * weight
            gd[rows] = (back * up * sig * (1.0 + gate * (1.0 - sig))).astype(BF16)
            ud[rows] = (back * act).astype(BF16)
            hwt[:, rows] = (hidden * weight).T.astype(BF16)
            return 0

        lax.fori_loop(0, NB, delta, 0)

    acc = pltpu.VMEM((ROWS, FF), F32)
    pl.run_scoped(forward_phase, acc, acc, acc)

    sent(meta, xss.at[NCH, 0])
    for j in range(NCH):
        sent(xr.at[j, :, pl.ds(0, CH)], xss.at[j, 0])
        sent(xr.at[j, :, pl.ds(CH, CH)], xss.at[j, 1])
    sent(zms.at[seven, rows_sent], zss.at[NCH])
    for j in (NCH - 2, NCH - 1):
        sent(zs.at[j % 2, seven, rows_sent], zss.at[j])

    def backward_phase(pg, pu, pd):
        p_all, ra, rb = (pg, pu, pd), (rag, rau, rad), (rbg, rbu, rbd)
        rx, outs = (rxg, rxu, rxd), (gate_out, up_out, down_out)

        def send_dots(b, _):
            @pl.when(b != me)
            def _():
                put(
                    zds.at[b, rows_sent], rdot.at[me, rows_sent], zts.at[NCH], ztr.at[NCH], peer(b)
                ).start()

            @pl.when(b == me)
            def _():
                rdot[b] = zds[b]

            return 0

        lax.fori_loop(0, NB, send_dots, 0)

        def index_of(q):
            ge2, ge6 = quo(q + 6, 8), quo(q + 2, 8)
            r = q + 6
            mid = 4 * (1 - (quo(r, 2) - 4)) + 1 + rem(r, 2)
            return (1 - ge2) * (7 - 4 * q) + (ge2 - ge6) * mid + ge6 * (4 * (7 - q))

        def compute(q):
            idx = index_of(q)
            slot, lanes = rem(quo(q, 2), 2), pl.ds(pl.multiple_of(rem(q, 2) * CH, CH), CH)

            @pl.when(q >= 4)
            def _():
                sent(zs.at[slot, seven, rows_sent, lanes], zts.at[q - 4])

            def input_rows(m, _):
                zz = rem(z + 1 + m, 4)
                rows = pl.ds(pl.multiple_of(zz * 2 * RB, 2 * RB), 2 * RB)
                out = nt(gd[rows], wg[idx]) + nt(ud[rows], wu[idx])
                zs[slot, pl.ds(zz * 2, 2), :, lanes] = out.astype(BF16).reshape(2, RB, CH)

                def start(b):
                    put(
                        zs.at[slot, b, rows_sent, lanes], ret.at[q, me, rows_sent],
                        zts.at[q], ztr.at[q], peer(b),
                    ).start()

                def own(b):
                    ret[q, b] = zs[slot, b, :, lanes]

                to_peers(start, own, zz)
                return 0

            lax.fori_loop(0, 4, input_rows, 0)
            toks = zr[idx, :, :, :CH].reshape(ROWS, CH)
            pg[q] = tn(toks, gd[...]).astype(BF16)
            pu[q] = tn(toks, ud[...]).astype(BF16)
            pd[q] = nn(hwt[...], zr[idx, :, :, CH:].reshape(ROWS, CH)).astype(BF16)

        def send_far(q, l):
            for n in range(3):
                size = p_all[n].shape[1] // 2
                for h in range(2):
                    put(
                        p_all[n].at[q, pl.ds(h * size, size)], ra[n].at[l, h],
                        ras.at[l, h, n], rar.at[l, h, n], ydir[h],
                    ).start()

        def send_near(q, l):
            for n in range(3):
                size = p_all[n].shape[1] // 2
                for h in range(2):
                    got(ra[n].at[l, h], rar.at[l, h, n])
                    rows = pl.ds(h * size, size)
                    p_all[n][q + h, rows] = (
                        p_all[n][q + h, rows].astype(F32) + ra[n][l, h].astype(F32)
                    ).astype(BF16)
                    put(
                        p_all[n].at[q + h], rb[n].at[l, h], rbs.at[l, h, n], rbr.at[l, h, n], ydir[h]
                    ).start()

        def gathered(q, l, n):
            for h in range(2):
                got(rb[n].at[l, h], rbr.at[l, h, n])
            return p_all[n][q].astype(F32) + rb[n][l, 0].astype(F32) + rb[n][l, 1].astype(F32)

        def back_rows(q):
            got(ret.at[q, seven, rows_sent], ztr.at[q])
            col = chunk_col(index_of(q))
            rows = ret[q].reshape(ROWS, CH)
            pown[q] = nn(gto[...], rows)
            og[:, pl.ds(col, CH)] = nn(gtp[...], rows).astype(BF16)
            put(og.at[:, pl.ds(col, CH)], xr2.at[q], xts.at[q], xtr.at[q], xfar).start()

        def step(q, _):
            compute(q)
            for l in (1, 0):

                @pl.when(q == 1 - l)
                def _():
                    send_far(1 - l, l)

                @pl.when(q == 5 - 2 * l)
                def _():
                    send_near(4 - 2 * l, l)

            @pl.when(q >= 4)
            def _():
                back_rows(q - 4)

            return 0

        lax.fori_loop(0, NCH, step, 0)

        def step_b(q, _):
            back_rows(q)
            return 0

        lax.fori_loop(4, NCH, step_b, 0)

        got(rdot.at[seven, rows_sent], ztr.at[NCH])
        dots = rdot[...].reshape(ROWS, 128)
        ddown[...] = nn(gto[...], dots)
        dpar[...] = nn(gtp[...], dots).astype(BF16)
        put(dpar, xdot, xts.at[NCH], xtr.at[NCH], xfar).start()

        for n in range(3):
            p_all[n][6] = gathered(6, 1, n).astype(BF16)
            put(p_all[n].at[6], rx[n], rxs.at[n], rxr.at[n], xnear).start()

        def finish(q, _):
            got(xr2.at[q], xtr.at[q])
            col = chunk_col(index_of(q))
            tk[:, pl.ds(col, CH)] = (pown[q] + xr2[q].astype(F32)).astype(BF16)
            return 0

        lax.fori_loop(0, NCH, finish, 0)
        whole = pltpu.make_async_copy(tk, token_out, osem.at[3])
        whole.start()
        got(xdot, xtr.at[NCH])
        all_dots = ddown[...] + xdot[...].astype(F32)
        lane_t = lax.broadcasted_iota(jnp.int32, (T, 128), 1)
        first = jnp.sum(jnp.where(lane_t == ids[:, 0:1], all_dots, 0.0), axis=1, keepdims=True)
        second = jnp.sum(jnp.where(lane_t == ids[:, 1:2], all_dots, 0.0), axis=1, keepdims=True)
        pick = lax.broadcasted_iota(jnp.int32, (T, 2), 1)
        route_out[...] = jnp.where(pick == 0, first, second).astype(BF16)

        last = [whole]
        for n in range(3):
            total = gathered(7, 0, n)
            got(rx[n], rxr.at[n])
            p_all[n][7] = (total + rx[n][...].astype(F32)).astype(BF16)
            cp = pltpu.make_async_copy(p_all[n].at[7], outs[n], osem.at[n])
            cp.start()
            last.append(cp)

        for idx in (1, 2, 4, 5, 6):
            for n in range(3):
                sent(w_all[n].at[idx], ags.at[idx, n, 0])
        for n in range(3):
            size = w_all[n].shape[1] // 2
            for h in range(2):
                for idx in (3, 7):
                    sent(w_all[n].at[idx, pl.ds(h * size, size)], ags.at[idx, n, h])
                for l in range(2):
                    sent(ra[n].at[l, h], ras.at[l, h, n])
                    sent(rb[n].at[l, h], rbs.at[l, h, n])
            sent(rx[n], rxs.at[n])
        sent(zds.at[seven, rows_sent], zts.at[NCH])
        for q in range(4, NCH):
            sent(zs.at[0, seven, rows_sent, pl.ds(0, CH)], zts.at[q])
        for q in range(NCH):
            sent(xr2.at[q], xts.at[q])
        sent(dpar, xts.at[NCH])
        for cp in last:
            cp.wait()

    pl.run_scoped(
        backward_phase,
        pltpu.VMEM((NCH, CH, FF), BF16),
        pltpu.VMEM((NCH, CH, FF), BF16),
        pltpu.VMEM((NCH, FF, CH), BF16),
    )


def on_device(tokens, out_grad, expert_ids, route_weight, w_gate, w_up, w_down):
    hbm = pl.BlockSpec(memory_space=pltpu.HBM)
    vmem = pltpu.VMEM
    sem = pltpu.SemaphoreType.DMA
    outs = pl.pallas_call(
        kernel,
        out_shape=(
            jax.ShapeDtypeStruct((T, D), BF16),
            jax.ShapeDtypeStruct((T, 2), BF16),
            jax.ShapeDtypeStruct((CH, FF), BF16),
            jax.ShapeDtypeStruct((CH, FF), BF16),
            jax.ShapeDtypeStruct((FF, CH), BF16),
        ),
        in_specs=[hbm] * 7,
        out_specs=(hbm, pl.BlockSpec(memory_space=vmem), hbm, hbm, hbm),
        scratch_shapes=[
            vmem((T, D), BF16), vmem((T, D), BF16), vmem((T, 2), jnp.int32), vmem((T, 2), BF16),
            vmem((T, 128), BF16), vmem((T, 128), BF16), vmem((NCH, T, 2 * CH), BF16),
            vmem((2, 128, T), F32), vmem((NB, RB, T), BF16), vmem((NB, RB, T), BF16),
            vmem((T, ROWS), BF16), vmem((T, ROWS), BF16),
            vmem((2, NB, RB, 2 * CH), BF16), vmem((NCH, NB, RB, 2 * CH), BF16),
            vmem((NB, RB, 128), BF16), vmem((NB, RB, 128), BF16),
            vmem((NCH, CH, FF), BF16), vmem((NCH, CH, FF), BF16), vmem((NCH, FF, CH), BF16),
            vmem((ROWS, FF), BF16), vmem((ROWS, FF), BF16), vmem((FF, ROWS), BF16),
            vmem((2, 2, CH // 2, FF), BF16), vmem((2, 2, CH // 2, FF), BF16),
            vmem((2, 2, FF // 2, CH), BF16),
            vmem((2, 2, CH, FF), BF16), vmem((2, 2, CH, FF), BF16), vmem((2, 2, FF, CH), BF16),
            vmem((CH, FF), BF16), vmem((CH, FF), BF16), vmem((FF, CH), BF16),
            vmem((NCH, NB, RB, CH), BF16), vmem((NB, RB, 128), BF16), vmem((NB, RB, 128), BF16),
            vmem((NCH, T, CH), F32), vmem((NCH, T, CH), BF16),
            vmem((T, 128), F32), vmem((T, 128), BF16), vmem((T, 128), BF16),
            sem((7,)), sem((4,)), sem((NCH + 1, 2)), sem((NCH + 1, 2)),
            sem((NCH + 1,)), sem((NCH + 1,)), sem((NCH, 3, 2)), sem((NCH, 3, 2)),
            sem((NCH + 1,)), sem((NCH + 1,)), sem((NCH + 1,)), sem((NCH + 1,)),
            sem((2, 2, 3)), sem((2, 2, 3)), sem((2, 2, 3)), sem((2, 2, 3)), sem((3,)), sem((3,)),
        ],
        compiler_params=pltpu.CompilerParams(
            collective_id=0, has_side_effects=True, vmem_limit_bytes=67043328
        ),
        name="routed_backward",
    )(
        tokens, out_grad, expert_ids, route_weight,
        w_gate.reshape(CH, FF), w_up.reshape(CH, FF), w_down.reshape(FF, CH),
    )
    token_grad, route_grad, gate, up, down = outs
    return token_grad, route_grad, gate[None], up[None], down[None]


def solution(mesh):
    placed = (
        P(("dp", "expert"), None),
        P(("dp", "expert"), None),
        P(("dp", "expert"), None),
        P(("dp", "expert"), None),
        P("expert", "dp", None),
        P("expert", "dp", None),
        P("expert", None, "dp"),
    )
    return jax.shard_map(
        on_device,
        mesh=mesh,
        in_specs=placed,
        out_specs=(
            P(("dp", "expert"), None),
            P(("dp", "expert"), None),
            P("expert", "dp", None),
            P("expert", "dp", None),
            P("expert", None, "dp"),
        ),
        check_vma=False,
    )
```

time: 564 us -> 220 us (0.39); the launches traced: 558 us -> 220 us
  waiting for transfers between devices: 253 us -> 0 us
  Pallas kernels: 0 us -> 210 us
  local copies, waits for them, and re-layouts: 146 us -> 9.33 us
  matrix products: 60.6 us -> 0 us
  other arithmetic: 50.7 us -> 0 us
  starting transfers between devices: 33 us -> 0 us
  between operations: 14.6 us -> 0.65 us
    all_to_all x4 -> x0, waiting for transfers between devices: 235 us -> none  [the longest x1 166 us: side_by_side(): lax.all_to_all(both, axis, split_axis=split_dim, concat_axis=concat_dim,...]
    pallas_call x0 -> x1, Pallas kernels: none -> 210 us  [on_device(): pl.pallas_call(kernel, out_shape=(jax.ShapeDtypeStruct((T, D), BF16), jax...]
    dot_general x9 -> x0, matrix products: 60.6 us -> none  [the longest x1 10.7 us: on_device(): jnp.einsum('erf,erd->efd', hidden, scaled, preferred_element_type=jnp.flo...]
    gather x6 -> x0, local copies, waits for them, and re-layouts: 37.9 us -> none  [the longest x2 15.3 us: on_device(): route_rows = back_rows.reshape(total_slots, model_width)[destination]]
    all_to_all x4 -> x0, starting transfers between devices: 32.4 us -> none  [the longest x1 9.28 us: on_device(): lax.all_to_all(send_weights, 'expert', split_axis=1, concat_axis=1, tiled...]
    unnamed x28 -> x13, local copies, waits for them, and re-layouts: 36.5 us -> 9.33 us
    unnamed x1 -> x0, other arithmetic: 25.2 us -> none
    convert_element_type x3 -> x0, local copies, waits for them, and re-layouts: 23.9 us -> none  [the longest x1 23.1 us: on_device(): input_grad = (jnp.einsum('erf,edf->erd', gate_delta, full_gate, preferred...]
  transfers between devices with their start and end apart: 8 -> 0, of which waited for: 4 -> 0; matrix products, arithmetic and copies ran while one was open for 42% -> 0% of each run, Pallas kernels for 0% -> 0%
where the time goes in v1:
time: 220 us
  Pallas kernels  210 us (95%)
  local copies, waits for them, and re-layouts  9.33 us (4%)
    pallas_call x1, Pallas kernels, on_device(): pl.pallas_call(kernel, out_shape=(jax.ShapeDtypeStruct((T, D), BF16), jax...  210 us
    unnamed x13, local copies, waits for them, and re-layouts  9.33 us

profile of v1, /device:TPU:1, one launch (start us, length us, event | category | flops | bytes accessed | tf_op | source)
XLA Modules:
  0.0 220.3 jit_solution(5086850599209661748)
XLA Ops:
  0.6 1.5 copy.13.rw_hbm
  2.1 1.5 copy.12.ids_hbm
  3.6 210.3 %routed_backward.1 = (bf16[320,2048]{1,0:T(8,128)(2,1)}, bf16[320,2]{1,0:T(8,128)(2,1)}, bf16[256,768]{1,0:T(8,128)(2,1)}, bf16[256,768]{1,0:T(8,128)(2,1)}, bf16[768,256]{1,0:T(8,128)(2,1)}) custom-call(bf16[320,2048]{1,0:T(8,128)(2,1)} %tokens_hbm.1, bf16[320,2048]{1,0:T(8,128)(2,1)} %grads_hbm.1, s32[320,2]{1,0:T(8,128)} %copy.12.ids_hbm, ...), custom_call_target="tpu_custom_call" | custom-call | tf_op jit(solution)/shard_map/routed_backward/pallas_call | solution.py:547
  213.9 1.5 copy.14
  215.4 0.0 copy-start.2
  215.4 0.0 copy-start.1
  215.4 2.6 %copy.19 = bf16[320,2048]{1,0:T(8,128)(2,1)} copy(bf16[320,2048]{1,0:T(8,128)(2,1)} %get-tuple-element.25) | data formatting | bytes 2621440
  218.0 0.0 copy-done.2
  218.0 0.0 copy-start
  218.0 0.7 copy.20
  218.8 0.0 copy-done.1
  218.8 0.7 copy.21
  219.5 0.0 copy-done
  219.5 0.7 copy.22
Async XLA Ops:
  215.4 2.6 %copy-start.2 = (bf16[256,768]{1,0:T(8,128)(2,1)S(1)}, bf16[256,768]{1,0:T(8,128)(2,1)}, u32[]{:S(2)}) copy-start(bf16[256,768]{1,0:T(8,128)(2,1)} %get-tuple-element.12) | copy-start | bytes 1179652
  215.4 3.3 %copy-start.1 = (bf16[256,768]{1,0:T(8,128)(2,1)S(1)}, bf16[256,768]{1,0:T(8,128)(2,1)}, u32[]{:S(2)}) copy-start(bf16[256,768]{1,0:T(8,128)(2,1)} %get-tuple-element.13) | copy-start | bytes 1179652
  218.0 1.5 copy-start
